TPU v7x, 32 devices: a whole 2x2x4 slice. The times are simulated.
32 devices in a mesh: dp: 8 (over z, x), mp: 4 (over y, core).
Axes of the slice: x: 2, y: 2, z: 4, core: 2. Of those that a mesh axis runs over, the one named last changes fastest.
Arguments:
- tokens: bfloat16 [8192, 2048], P('dp', 'mp'), may hold values from -6 to 6
- norm_gain: bfloat16 [2048], replicated, may hold values from 0.099609375 to 1.8984375
- wi_gate: bfloat16 [2048, 5120], P(None, 'mp'), may hold values from -0.125 to 0.125
- wi_linear: bfloat16 [2048, 5120], P(None, 'mp'), may hold values from -0.125 to 0.125
- wo_out: bfloat16 [5120, 2048], P('mp'), may hold values from -0.078125 to 0.078125
- task_table: float32 [8, 64], replicated, may hold values from -5 to 5
- layer_table: float32 [24, 64], replicated, may hold values from -5 to 5
- task_ids: int32 [64], P('dp'), may hold values from 0 to 7
- layer_index: int32 [1], replicated, may hold values from 0 to 23
- hyper_in: bfloat16 [128, 1024], P(None, 'mp'), may hold values from -0.5 to 0.5
- gen_down: bfloat16 [1024, 131072], P(None, ('mp', 'dp')), may hold values from -0.0078125 to 0.0078125
- gen_up: bfloat16 [1024, 131072], P(None, ('mp', 'dp')), may hold values from -0.046875 to 0.046875
Outputs:
- mixed: bfloat16 [8192, 2048], P('dp', 'mp')
All inputs are finite; a program needn't handle non-finite values.
Results may differ from a plain program's by a relative error of at most 0.019.
Values may be sent and summed in bfloat16 or wider, within the bound.
A program may use at most 128 MiB of HBM per device.

v0:
```python
import jax
import jax.numpy as jnp
from jax import lax
from jax.sharding import PartitionSpec as P

R = 64


def matmul(left, right):
    return jnp.dot(left, right, preferred_element_type=jnp.float32)


def per_device(
    tokens,
    norm_gain,
    wi_gate,
    wi_linear,
    wo_out,
    task_table,
    layer_table,
    task_ids,
    layer_index,
    hyper_in,
    gen_down,
    gen_up,
):
    task_count = task_table.shape[0]
    layer_row = jnp.take(layer_table, layer_index, axis=0)
    embed = jnp.concatenate(
        [task_table, jnp.broadcast_to(layer_row, (task_count, layer_row.shape[1]))], axis=1
    ).astype(jnp.bfloat16)
    hidden_part = jnp.maximum(matmul(embed, hyper_in), 0.0).astype(jnp.bfloat16)
    hidden = lax.all_gather(hidden_part, "mp", axis=1, tiled=True)
    every_id = lax.all_gather(task_ids, "dp", axis=0, tiled=True)
    wanted = jnp.take(hidden, every_id, axis=0)
    made = (
        matmul(wanted, gen_down).astype(jnp.bfloat16),
        matmul(wanted, gen_up).astype(jnp.bfloat16),
    )
    local_down, local_up = (
        lax.all_to_all(made[0], "dp", split_axis=0, concat_axis=1, tiled=True),
        lax.all_to_all(made[1], "dp", split_axis=0, concat_axis=1, tiled=True),
    )
    full_rows = lax.all_gather(tokens, "mp", axis=1, tiled=True)
    wide = full_rows.astype(jnp.float32)
    scale = lax.rsqrt(jnp.mean(wide * wide, axis=-1, keepdims=True) + 1e-06)
    normed = (wide * scale * norm_gain.astype(jnp.float32)).astype(jnp.bfloat16)
    gate = matmul(normed, wi_gate)
    linear = matmul(normed, wi_linear)
    act = (jax.nn.gelu(gate, approximate=True) * linear).astype(jnp.bfloat16)
    seqs_dev = task_ids.shape[0]
    tok_dev = tokens.shape[0]
    seq_len = tok_dev // seqs_dev
    partial_sums = matmul(act, wo_out)
    ffout = lax.psum_scatter(
        partial_sums.astype(jnp.bfloat16), "mp", scatter_dimension=1, tiled=True
    )
    down_block = local_down.reshape(seqs_dev, -1, R)
    up_block = local_up.reshape(seqs_dev, -1, R)
    blocks = ffout.reshape(seqs_dev, seq_len, -1)
    squeeze_part = jnp.einsum(
        "std,sdr->str", blocks, down_block, preferred_element_type=jnp.float32
    )
    squeeze_full = lax.psum(squeeze_part.astype(jnp.bfloat16), "mp").astype(jnp.float32)
    squeezed = jnp.maximum(squeeze_full, 0.0).astype(jnp.bfloat16)
    expand = jnp.einsum("str,sdr->std", squeezed, up_block, preferred_element_type=jnp.float32)
    total = tokens.astype(jnp.float32) + ffout.astype(jnp.float32) + expand.reshape(tok_dev, -1)
    return total.astype(jnp.bfloat16)


def solution(mesh):
    return jax.shard_map(
        per_device,
        mesh=mesh,
        in_specs=(
            P("dp", "mp"),
            P(),
            P(None, "mp"),
            P(None, "mp"),
            P("mp", None),
            P(),
            P(),
            P("dp"),
            P(),
            P(None, "mp"),
            P(None, ("mp", "dp")),
            P(None, ("mp", "dp")),
        ),
        out_specs=P("dp", "mp"),
        check_vma=False,
    )
```

profile of v0, /device:TPU:0, one launch (start us, length us, event | category | flops | bytes accessed | tf_op | source)
XLA Modules:
  0.0 174.6 jit_solution(7065484068272233757)
XLA Ops:
  6.5 0.0 copy-start
  6.5 0.0 all-gather.2.cloned.1.call-start
  6.5 0.7 all-gather.2.cloned.1.call-update
  7.3 0.0 reduce-scatter.2.cloned.1.call-start
  7.3 0.7 convert_element_type.45
  8.0 38.1 %all-gather.2.cloned.1.call-done = bf16[1024,2048]{1,0:T(8,128)(2,1)} async-done(((bf16[1024,512]{1,0:T(8,128)(2,1)}), bf16[1024,2048]{1,0:T(8,128)(2,1)}) %all-gather.2.cloned.1.call-update) | async-done | bytes 4194320 | tf_op jit(solution)/shard_map/all_gather | solution.py:44
  46.1 3.1 %fusion = f32[1024]{0:T(1024)S(1)} fusion(bf16[1024,2048]{1,0:T(8,128)(2,1)} %all-gather.2.cloned.1.call-done), kind=kLoop, calls=%fused_computation.3 | loop fusion | flops 6290432 | bytes 4198400 | tf_op jit(solution)/shard_map/reduce_sum | solution.py:46
  49.2 10.7 %fusion.16 = f32[1024,1280]{1,0:T(8,128)} fusion(bf16[2048,1280]{1,0:T(8,128)(2,1)} %param.14, bf16[1024,2048]{1,0:T(8,128)(2,1)} %all-gather.2.cloned.1.call-done, f32[2048]{0:T(1024)S(1)} %convert_element_type.45, f32[1024]{0:T(1024)S(1)} %add_rsqrt_fusion), kind=kOutput, calls=%fused_computation.23 | convolution fusion | flops 5377097728 | bytes 14692352 | tf_op jit(solution)/shard_map/dot_general | solution.py:10
  59.9 0.0 copy-start.3
  59.9 0.0 copy-start.5
  59.9 0.0 copy-start.4
  59.9 19.9 %convolution_convert_fusion.2 = bf16[1024,2048]{1,0:T(8,128)(2,1)} fusion(bf16[1280,2048]{1,0:T(8,128)(2,1)} %param.16, f32[1024,1280]{1,0:T(8,128)} %fusion.16, bf16[2048,1280]{1,0:T(8,128)(2,1)} %param.15, bf16[1024,2048]{1,0:T(8,128)(2,1)} %all-gather.2.cloned.1.call-done, f32[2048]{0:T(1024)S(1)} %convert_element_type.45, f32[1024]{0:T(1024)S(1)} %add_rsqrt_fusion), kind=kOutput, calls=%fused_computation.20 | convolution fusion | flops 10761011200 | bytes 24129536 | tf_op jit(solution)/shard_map/dot_general | solution.py:10
  79.8 0.0 reduce-scatter.2.cloned.1.call-update
  80.5 0.0 copy-done.3
  80.5 0.7 fusion.27
  81.2 0.1 pad.3.clone
  81.3 0.0 copy-done.5
  81.3 0.6 dynamic-slice.4
  82.6 0.0 copy-done.4
  82.6 0.2 dynamic-update-slice.1
  82.8 11.4 %all-reduce = s32[64]{0:T(128)S(1)} all-reduce(s32[64]{0:T(128)S(1)} %dynamic-update-slice.1), channel_id=1, replica_groups=mesh['dp'=8,'mp'=4] {'dp'}, use_global_device_ids=true, to_apply=%add | all-reduce | flops 64 | bytes 512
  94.2 0.0 copy-done
  94.2 0.1 fusion.18
  94.3 5.2 %all_gather.11 = bf16[8,1024]{1,0:T(8,128)(2,1)S(1)} all-gather(bf16[8,256]{1,0:T(8,128)(2,1)S(1)} %fusion.18), channel_id=1, replica_groups=mesh['dp'=8,'mp'=4] {'mp'}, dimensions={1}, use_global_device_ids=true | all-gather | bytes 20480 | tf_op jit(solution)/shard_map/all_gather | solution.py:33
  99.5 0.7 gather_fusion
  100.2 5.8 %fusion.12 = bf16[8,8,4096]{2,1,0:T(8,128)(2,1)} fusion(bf16[1024,4096]{1,0:T(8,128)(2,1)} %param.22, bf16[64,1024]{1,0:T(8,128)(2,1)S(1)} %gather_fusion, pred[64]{0:T(512)(128)(4,1)S(1)} %compare_and_fusion), kind=kOutput, calls=%fused_computation.18 | convolution fusion | flops 537198592 | bytes 9044032 | tf_op jit(solution)/shard_map/dot_general | solution.py:10
  106.1 3.5 %all-to-all-start = ((bf16[8,8,4096]{2,1,0:T(8,128)(2,1)}), bf16[8,8,4096]{2,1,0:T(8,128)(2,1)S(1)}, u32[]{:S(2)}, u32[]{:S(2)}) async-start(bf16[8,8,4096]{2,1,0:T(8,128)(2,1)} %fusion.12), calls=%async_computation.1 | async-start | bytes 1048576 | tf_op jit(solution)/shard_map/all_to_all | solution.py:41
  109.6 5.8 %fusion.13 = bf16[8,8,4096]{2,1,0:T(8,128)(2,1)} fusion(bf16[1024,4096]{1,0:T(8,128)(2,1)} %param.23, bf16[64,1024]{1,0:T(8,128)(2,1)S(1)} %gather_fusion, pred[64]{0:T(512)(128)(4,1)S(1)} %compare_and_fusion), kind=kOutput, calls=%fused_computation.19 | convolution fusion | flops 537198592 | bytes 9044032 | tf_op jit(solution)/shard_map/dot_general | solution.py:10
  115.4 9.4 %all-to-all-done = bf16[8,8,4096]{2,1,0:T(8,128)(2,1)S(1)} async-done(((bf16[8,8,4096]{2,1,0:T(8,128)(2,1)}), bf16[8,8,4096]{2,1,0:T(8,128)(2,1)S(1)}, u32[]{:S(2)}, u32[]{:S(2)}) %all-to-all-start) | async-done | bytes 524320 | tf_op jit(solution)/shard_map/all_to_all | solution.py:41
  124.8 4.3 %all-to-all-start.1 = ((bf16[8,8,4096]{2,1,0:T(8,128)(2,1)}), bf16[8,8,4096]{2,1,0:T(8,128)(2,1)}, u32[]{:S(2)}, u32[]{:S(2)}) async-start(bf16[8,8,4096]{2,1,0:T(8,128)(2,1)} %fusion.13), calls=%async_computation.2 | async-start | bytes 1048576 | tf_op jit(solution)/shard_map/all_to_all | solution.py:42
  129.1 0.0 all-reduce.3.cloned.1.call-start
  129.1 0.0 copy-start.1
  129.1 0.3 copy.16
  129.4 1.1 reshape.46
  130.6 0.0 reduce-scatter.2.cloned.1.call-done
  130.6 0.0 copy-start.2
  130.6 2.5 %convolution_convert_fusion.3 = bf16[8,128,64]{1,2,0:T(8,128)(2,1)} fusion(bf16[8,128,512]{2,1,0:T(8,128)(2,1)} %bitcast.25, bf16[8,512,64]{2,1,0:T(8,128)(2,1)S(1)} %reshape.46), kind=kOutput, calls=%fused_computation.24 | convolution fusion | flops 67174400 | bytes 1703936 | tf_op jit(solution)/shard_map/std,sdr->str/dot_general | solution.py:61
  133.1 0.0 all-reduce.3.cloned.1.call-update
  133.1 10.2 %all-to-all-done.1 = bf16[8,8,4096]{2,1,0:T(8,128)(2,1)} async-done(((bf16[8,8,4096]{2,1,0:T(8,128)(2,1)}), bf16[8,8,4096]{2,1,0:T(8,128)(2,1)}, u32[]{:S(2)}, u32[]{:S(2)}) %all-to-all-start.1) | async-done | bytes 524320 | tf_op jit(solution)/shard_map/all_to_all | solution.py:42
  143.3 2.1 %copy.18 = bf16[8,8,4096]{2,1,0:T(8,128)(2,1)} copy(bf16[8,8,4096]{2,0,1:T(8,128)(2,1)} %bitcast.8) | data formatting | bytes 1048576 | tf_op jit(solution)/shard_map/all_to_all | solution.py:42
  145.4 2.1 %reshape.47 = bf16[8,512,64]{2,1,0:T(8,128)(2,1)S(1)} reshape(bf16[8,8,4096]{2,1,0:T(8,128)(2,1)} %copy.18) | data formatting | bytes 1048576 | tf_op jit(solution)/shard_map/reshape | solution.py:59
  147.5 17.7 %all-reduce.3.cloned.1.call-done = bf16[8,128,64]{1,2,0:T(8,128)(2,1)} async-done(((bf16[8,128,64]{1,2,0:T(8,128)(2,1)}), bf16[8,128,64]{1,2,0:T(8,128)(2,1)}) %all-reduce.3.cloned.1.call-update) | async-done | bytes 131088 | tf_op jit(solution)/shard_map/psum | solution.py:64
  165.2 1.4 fusion.21
  166.6 0.0 copy-done.1
  166.6 0.0 copy-done.2
  166.6 1.4 fusion.14
  (6 shorter events, 0.0 us)
Async XLA Ops:
  6.5 87.6 %copy-start = (bf16[128,256]{1,0:T(8,128)(2,1)S(1)}, bf16[128,256]{1,0:T(8,128)(2,1)}, u32[]{:S(2)}) copy-start(bf16[128,256]{1,0:T(8,128)(2,1)} %param.21) | copy-start | bytes 196612
  6.5 39.6 %all-gather.2.cloned.1.call-start = ((), (), s32[]{:S(2)}) async-start(), calls=%async_computation.3 | async-start | bytes 5242880 | tf_op jit(solution)/shard_map/all_gather | solution.py:44
  7.3 123.3 %reduce-scatter.2.cloned.1.call-start = ((), (), s32[]{:S(2)}) async-start(), calls=%async_computation.4 | async-start | bytes 5242880 | tf_op jit(solution)/shard_map/reduce_scatter | solution.py:55
  59.9 20.6 %copy-start.3 = (f32[8,64]{1,0:T(8,128)S(1)}, f32[8,64]{1,0:T(8,128)}, u32[]{:S(2)}) copy-start(f32[8,64]{1,0:T(8,128)} %param.17) | copy-start | bytes 6148
  59.9 21.4 %copy-start.5 = (u32[32]{0:T(128)S(1)}, u32[32]{0:T(128)}, u32[]{:S(2)}) copy-start(u32[32]{0:T(128)} %constant.73) | copy-start | bytes 388
  59.9 22.7 %copy-start.4 = (s32[8]{0:T(128)S(1)}, s32[8]{0:T(128)}, u32[]{:S(2)}) copy-start(s32[8]{0:T(128)} %param.19) | copy-start | bytes 100
  106.1 18.7 %all-to-all-start = ((bf16[8,8,4096]{2,1,0:T(8,128)(2,1)}), bf16[8,8,4096]{2,1,0:T(8,128)(2,1)S(1)}, u32[]{:S(2)}, u32[]{:S(2)}) async-start(bf16[8,8,4096]{2,1,0:T(8,128)(2,1)} %fusion.12), calls=%async_computation.1 | async-start | bytes 1048576 | tf_op jit(solution)/shard_map/all_to_all | solution.py:41
  124.8 18.6 %all-to-all-start.1 = ((bf16[8,8,4096]{2,1,0:T(8,128)(2,1)}), bf16[8,8,4096]{2,1,0:T(8,128)(2,1)}, u32[]{:S(2)}, u32[]{:S(2)}) async-start(bf16[8,8,4096]{2,1,0:T(8,128)(2,1)} %fusion.13), calls=%async_computation.2 | async-start | bytes 1048576 | tf_op jit(solution)/shard_map/all_to_all | solution.py:42
  129.1 36.1 %all-reduce.3.cloned.1.call-start = ((), (), s32[]{:S(2)}) async-start(), calls=%async_computation.5 | async-start | bytes 262144 | tf_op jit(solution)/shard_map/psum | solution.py:64
  129.1 37.5 %copy-start.1 = (bf16[1024,512]{1,0:T(8,128)(2,1)S(1)}, bf16[1024,512]{1,0:T(8,128)(2,1)}, u32[]{:S(2)}) copy-start(bf16[1024,512]{1,0:T(8,128)(2,1)} %param.12) | copy-start | bytes 3145732
  130.6 36.0 %copy-start.2 = (bf16[1024,512]{1,0:T(8,128)(2,1)S(1)}, bf16[1024,512]{1,0:T(8,128)(2,1)}, u32[]{:S(2)}) copy-start(bf16[1024,512]{1,0:T(8,128)(2,1)} %reduce-scatter.2.cloned.1.call-done) | copy-start | bytes 3145732
Sparse Core Ops, SparseCore 0:
  8.9 37.1 all-gather.1
  80.0 44.3 reduce-scatter.1
  133.2 31.9 all-reduce.2
where the time goes:
time: 175 us
  waiting for transfers between devices  76.2 us (44%)
  matrix products  46.2 us (26%)
  blocking collectives  16.6 us (9%)
  between operations  14.6 us (8%)
  starting transfers between devices  7.9 us (5%)
  local copies, waits for them, and re-layouts  7.23 us (4%)
  other arithmetic  5.92 us (3%)
    dot_general x5, matrix products, matmul(): return jnp.dot(left, right, preferred_element_type=jnp.float32)  42.4 us
    all_gather x1, waiting for transfers between devices, per_device(): full_rows = lax.all_gather(tokens, 'mp', axis=1, tiled=True)  38.1 us
    psum x1, waiting for transfers between devices, per_device(): lax.psum(squeeze_part.astype(jnp.bfloat16), 'mp').astype(jnp.float32)  17.7 us
    unnamed x1, blocking collectives  11.4 us
    all_to_all x1, waiting for transfers between devices, per_device(): lax.all_to_all(made[1], 'dp', split_axis=0, concat_axis=1, tiled=True)  10.2 us
    all_to_all x1, waiting for transfers between devices, per_device(): lax.all_to_all(made[0], 'dp', split_axis=0, concat_axis=1, tiled=True)  9.39 us
    all_gather x1, blocking collectives, per_device(): hidden = lax.all_gather(hidden_part, 'mp', axis=1, tiled=True)  5.2 us
    all_to_all x1, starting transfers between devices, per_device(): lax.all_to_all(made[1], 'dp', split_axis=0, concat_axis=1, tiled=True)  4.33 us
  transfers between devices with their start and end apart: 5, of which 4 were waited for; matrix products, arithmetic and copies ran while one was open for 13% of the time, Pallas kernels for 0%

commit v1 on v0

--- a/solution.py
+++ b/solution.py
@@ -38,7 +38,10 @@
         matmul(wanted, gen_up).astype(jnp.bfloat16),
     )
     local_down, local_up = (
-        lax.all_to_all(made[0], "dp", split_axis=0, concat_axis=1, tiled=True),
+        jnp.concatenate(
+            lax.all_to_all(jnp.stack(jnp.split(made[0], lax.axis_size("dp"), axis=0)), "dp", 0, 0),
+            axis=1,
+        ),
         lax.all_to_all(made[1], "dp", split_axis=0, concat_axis=1, tiled=True),
     )
     full_rows = lax.all_gather(tokens, "mp", axis=1, tiled=True)

time: 175 us -> 169 us (0.966)
  waiting for transfers between devices: 76.2 us -> 59.7 us
  local copies, waits for them, and re-layouts: 7.23 us -> 13.5 us
  starting transfers between devices: 7.9 us -> 9.93 us
  blocking collectives: 16.6 us -> 18.5 us
    all_gather x1, waiting for transfers between devices: 38.1 us -> 8.93 us  [per_device(): full_rows = lax.all_gather(tokens, 'mp', axis=1, tiled=True)]
    reduce_scatter x1, waiting for transfers between devices: 0.02 us -> 13.3 us  [per_device(): lax.psum_scatter(partial_sums.astype(jnp.bfloat16), 'mp', scatter_dimensi...]
    all_to_all x1, waiting for transfers between devices: 10.2 us -> 0.01 us  [per_device(): lax.all_to_all(made[1], 'dp', split_axis=0, concat_axis=1, tiled=True)]
    psum x1, waiting for transfers between devices: 17.7 us -> 27.7 us  [per_device(): lax.psum(squeeze_part.astype(jnp.bfloat16), 'mp').astype(jnp.float32)]
    unnamed x15 -> x16, local copies, waits for them, and re-layouts: 0.85 us -> 6.51 us
    all_to_all x1, starting transfers between devices: 3.49 us -> 5.51 us  [per_device(): lax.all_to_all(jnp.stack(jnp.split(made[0], lax.axis_size('dp'), axis=0))...]
    another operation x0 -> x2, local copies, waits for them, and re-layouts: none -> 1.75 us  [the longest x1 1.12 us: per_device(): down_block = local_down.reshape(seqs_dev, -1, R)]
  transfers between devices with their start and end apart: 5 -> 5, of which waited for: 4 -> 4; matrix products, arithmetic and copies ran while one was open for 13% -> 17% of each run, Pallas kernels for 0% -> 0%
where the time goes in v1:
time: 169 us; the launch traced here: 168 us
  waiting for transfers between devices  59.7 us (35%)
  matrix products  45.6 us (27%)
  blocking collectives  18.5 us (11%)
  between operations  14.5 us (9%)
  local copies, waits for them, and re-layouts  13.5 us (8%)
  starting transfers between devices  9.93 us (6%)
  other arithmetic  6.59 us (4%)
    dot_general x5, matrix products, matmul(): return jnp.dot(left, right, preferred_element_type=jnp.float32)  41.7 us
    psum x1, waiting for transfers between devices, per_device(): lax.psum(squeeze_part.astype(jnp.bfloat16), 'mp').astype(jnp.float32)  27.7 us
    reduce_scatter x1, waiting for transfers between devices, per_device(): lax.psum_scatter(partial_sums.astype(jnp.bfloat16), 'mp', scatter_dimensi...  13.3 us
    unnamed x1, blocking collectives  13.1 us
    all_to_all x1, waiting for transfers between devices, per_device(): lax.all_to_all(jnp.stack(jnp.split(made[0], lax.axis_size('dp'), axis=0))...  8.98 us
    all_gather x1, waiting for transfers between devices, per_device(): full_rows = lax.all_gather(tokens, 'mp', axis=1, tiled=True)  8.93 us
    unnamed x16, local copies, waits for them, and re-layouts  6.51 us
    all_to_all x1, starting transfers between devices, per_device(): lax.all_to_all(jnp.stack(jnp.split(made[0], lax.axis_size('dp'), axis=0))...  5.51 us
  transfers between devices with their start and end apart: 5, of which 4 were waited for; matrix products, arithmetic and copies ran while one was open for 17% of the time, Pallas kernels for 0%

profile of v1, /device:TPU:0, one launch (start us, length us, event | category | flops | bytes accessed | tf_op | source)
XLA Modules:
  0.0 168.3 jit_solution(17253520479198952439)
XLA Ops:
  6.5 0.0 copy-start
  6.5 0.0 all-gather.2.cloned.1.call-start
  6.5 0.7 all-gather.2.cloned.1.call-update
  7.3 0.0 reduce-scatter.2.cloned.1.call-start
  8.0 0.7 convert.7
  8.7 0.7 convert_element_type.45
  9.3 0.7 fusion.34
  10.0 0.1 pad.3.clone
  10.1 1.2 dynamic-slice.4
  12.0 0.9 dynamic-update-slice.1
  12.9 13.1 %all-reduce = s32[64]{0:T(128)S(1)} all-reduce(s32[64]{0:T(128)S(1)} %dynamic-update-slice.1), channel_id=1, replica_groups=mesh['dp'=8,'mp'=4] {'dp'}, use_global_device_ids=true, to_apply=%add | all-reduce | flops 64 | bytes 512
  26.0 0.0 copy-done
  26.0 0.1 fusion.17
  26.1 5.4 %all_gather.11 = bf16[8,1024]{1,0:T(8,128)(2,1)S(1)} all-gather(bf16[8,256]{1,0:T(8,128)(2,1)S(1)} %fusion.17), channel_id=1, replica_groups=mesh['dp'=8,'mp'=4] {'mp'}, dimensions={1}, use_global_device_ids=true | all-gather | bytes 20480 | tf_op jit(solution)/shard_map/all_gather | solution.py:33
  31.5 0.7 gather_fusion
  32.2 5.1 %convolution_convert_fusion.1 = bf16[64,4096]{1,0:T(8,128)(2,1)S(1)} fusion(bf16[1024,4096]{1,0:T(8,128)(2,1)} %param.22, bf16[64,1024]{1,0:T(8,128)(2,1)S(1)} %gather_fusion, pred[64]{0:T(512)(128)(4,1)S(1)} %compare_and_fusion), kind=kOutput, calls=%fused_computation.17 | convolution fusion | flops 537198592 | bytes 9044032 | tf_op jit(solution)/shard_map/dot_general | solution.py:10
  37.3 8.9 %all-gather.2.cloned.1.call-done = bf16[1024,2048]{1,0:T(8,128)(2,1)} async-done(((bf16[1024,512]{1,0:T(8,128)(2,1)}), bf16[1024,2048]{1,0:T(8,128)(2,1)}) %all-gather.2.cloned.1.call-update) | async-done | bytes 4194320 | tf_op jit(solution)/shard_map/all_gather | solution.py:47
  46.2 3.1 %fusion = f32[1024]{0:T(1024)S(1)} fusion(bf16[1024,2048]{1,0:T(8,128)(2,1)} %all-gather.2.cloned.1.call-done), kind=kLoop, calls=%fused_computation.3 | loop fusion | flops 6290432 | bytes 4198400 | tf_op jit(solution)/shard_map/reduce_sum | solution.py:49
  49.3 10.7 %fusion.15 = f32[1024,1280]{1,0:T(8,128)} fusion(bf16[2048,1280]{1,0:T(8,128)(2,1)} %param.14, bf16[1024,2048]{1,0:T(8,128)(2,1)} %all-gather.2.cloned.1.call-done, f32[2048]{0:T(1024)S(1)} %convert_element_type.45, f32[1024]{0:T(1024)S(1)} %add_rsqrt_fusion), kind=kOutput, calls=%fused_computation.22 | convolution fusion | flops 5377097728 | bytes 14692352 | tf_op jit(solution)/shard_map/dot_general | solution.py:10
  60.0 19.9 %convolution_convert_fusion.2 = bf16[1024,2048]{1,0:T(8,128)(2,1)} fusion(bf16[1280,2048]{1,0:T(8,128)(2,1)} %param.16, f32[1024,1280]{1,0:T(8,128)} %fusion.15, bf16[2048,1280]{1,0:T(8,128)(2,1)} %param.15, bf16[1024,2048]{1,0:T(8,128)(2,1)} %all-gather.2.cloned.1.call-done, f32[2048]{0:T(1024)S(1)} %convert_element_type.45, f32[1024]{0:T(1024)S(1)} %add_rsqrt_fusion), kind=kOutput, calls=%fused_computation.19 | convolution fusion | flops 10761011200 | bytes 24129536 | tf_op jit(solution)/shard_map/dot_general | solution.py:10
  79.9 0.0 reduce-scatter.2.cloned.1.call-update
  79.9 0.6 fusion.29
  80.5 0.6 fusion.28
  81.2 0.6 fusion.27
  81.8 0.6 fusion.26
  82.4 0.6 fusion.25
  83.1 0.6 fusion.24
  83.7 0.6 fusion.23
  84.3 0.6 fusion.22
  85.0 5.5 %all-to-all-start = ((bf16[8,8,4096]{2,1,0:T(8,128)(2,1)}), bf16[8,8,4096]{2,1,0:T(8,128)(2,1)S(1)}, u32[]{:S(2)}, u32[]{:S(2)}) async-start(bf16[8,8,4096]{2,1,0:T(8,128)(2,1)} %fusion.22), calls=%async_computation.1 | async-start | bytes 1048576 | tf_op jit(solution)/shard_map/all_to_all | solution.py:42
  90.5 5.9 %fusion.12 = bf16[8,8,4096]{2,1,0:T(8,128)(2,1)} fusion(bf16[1024,4096]{1,0:T(8,128)(2,1)} %param.23, bf16[64,1024]{1,0:T(8,128)(2,1)S(1)} %gather_fusion, pred[64]{0:T(512)(128)(4,1)S(1)} %compare_and_fusion), kind=kOutput, calls=%fused_computation.18 | convolution fusion | flops 537198592 | bytes 9044032 | tf_op jit(solution)/shard_map/dot_general | solution.py:10
  96.4 9.0 %all-to-all-done = bf16[8,8,4096]{2,1,0:T(8,128)(2,1)S(1)} async-done(((bf16[8,8,4096]{2,1,0:T(8,128)(2,1)}), bf16[8,8,4096]{2,1,0:T(8,128)(2,1)S(1)}, u32[]{:S(2)}, u32[]{:S(2)}) %all-to-all-start) | async-done | bytes 524320 | tf_op jit(solution)/shard_map/all_to_all | solution.py:42
  105.3 4.3 %all-to-all-start.1 = ((bf16[8,8,4096]{2,1,0:T(8,128)(2,1)}), bf16[8,8,4096]{2,1,0:T(8,128)(2,1)}, u32[]{:S(2)}, u32[]{:S(2)}) async-start(bf16[8,8,4096]{2,1,0:T(8,128)(2,1)} %fusion.12), calls=%async_computation.2 | async-start | bytes 1048576 | tf_op jit(solution)/shard_map/all_to_all | solution.py:45
  109.7 0.0 all-reduce.3.cloned.1.call-start
  109.7 0.0 copy-start.1
  109.7 0.3 copy.16
  110.0 1.1 reshape_reshape.3
  111.2 13.3 %reduce-scatter.2.cloned.1.call-done = bf16[1024,512]{1,0:T(8,128)(2,1)} async-done(((bf16[1024,2048]{1,0:T(8,128)(2,1)}), bf16[1024,512]{1,0:T(8,128)(2,1)}) %reduce-scatter.2.cloned.1.call-update) | async-done | bytes 1048592 | tf_op jit(solution)/shard_map/reduce_scatter | solution.py:58
  124.5 2.5 %convolution_convert_fusion.3 = bf16[8,128,64]{1,2,0:T(8,128)(2,1)} fusion(bf16[8,128,512]{2,1,0:T(8,128)(2,1)} %bitcast.55, bf16[8,512,64]{2,1,0:T(8,128)(2,1)S(1)} %reshape_reshape.3), kind=kOutput, calls=%fused_computation.23 | convolution fusion | flops 67174400 | bytes 1703936 | tf_op jit(solution)/shard_map/std,sdr->str/dot_general | solution.py:64
  127.0 0.0 all-reduce.3.cloned.1.call-update
  127.0 0.0 all-to-all-done.1
  127.0 2.1 %copy.18 = bf16[8,8,4096]{2,1,0:T(8,128)(2,1)} copy(bf16[8,8,4096]{2,0,1:T(8,128)(2,1)} %bitcast.15) | data formatting | bytes 1048576 | tf_op jit(solution)/shard_map/all_to_all | solution.py:45
  129.1 2.1 %reshape.43 = bf16[8,512,64]{2,1,0:T(8,128)(2,1)S(1)} reshape(bf16[8,8,4096]{2,1,0:T(8,128)(2,1)} %copy.18) | data formatting | bytes 1048576 | tf_op jit(solution)/shard_map/reshape | solution.py:62
  131.2 27.7 %all-reduce.3.cloned.1.call-done = bf16[8,128,64]{1,2,0:T(8,128)(2,1)} async-done(((bf16[8,128,64]{1,2,0:T(8,128)(2,1)}), bf16[8,128,64]{1,2,0:T(8,128)(2,1)}) %all-reduce.3.cloned.1.call-update) | async-done | bytes 131088 | tf_op jit(solution)/shard_map/psum | solution.py:67
  158.9 1.4 fusion.20
  160.3 0.0 copy-done.1
  160.3 0.0 copy-done.2
  160.3 1.4 fusion.13
  (6 shorter events, 0.0 us)
Async XLA Ops:
  6.5 19.4 %copy-start = (bf16[128,256]{1,0:T(8,128)(2,1)S(1)}, bf16[128,256]{1,0:T(8,128)(2,1)}, u32[]{:S(2)}) copy-start(bf16[128,256]{1,0:T(8,128)(2,1)} %param.21) | copy-start | bytes 196612
  6.5 39.7 %all-gather.2.cloned.1.call-start = ((), (), s32[]{:S(2)}) async-start(), calls=%async_computation.3 | async-start | bytes 5242880 | tf_op jit(solution)/shard_map/all_gather | solution.py:47
  7.3 117.2 %reduce-scatter.2.cloned.1.call-start = ((), (), s32[]{:S(2)}) async-start(), calls=%async_computation.4 | async-start | bytes 5242880 | tf_op jit(solution)/shard_map/reduce_scatter | solution.py:58
  85.0 20.4 %all-to-all-start = ((bf16[8,8,4096]{2,1,0:T(8,128)(2,1)}), bf16[8,8,4096]{2,1,0:T(8,128)(2,1)S(1)}, u32[]{:S(2)}, u32[]{:S(2)}) async-start(bf16[8,8,4096]{2,1,0:T(8,128)(2,1)} %fusion.22), calls=%async_computation.1 | async-start | bytes 1048576 | tf_op jit(solution)/shard_map/all_to_all | solution.py:42
  105.3 21.6 %all-to-all-start.1 = ((bf16[8,8,4096]{2,1,0:T(8,128)(2,1)}), bf16[8,8,4096]{2,1,0:T(8,128)(2,1)}, u32[]{:S(2)}, u32[]{:S(2)}) async-start(bf16[8,8,4096]{2,1,0:T(8,128)(2,1)} %fusion.12), calls=%async_computation.2 | async-start | bytes 1048576 | tf_op jit(solution)/shard_map/all_to_all | solution.py:45
  109.7 49.2 %all-reduce.3.cloned.1.call-start = ((), (), s32[]{:S(2)}) async-start(), calls=%async_computation.5 | async-start | bytes 262144 | tf_op jit(solution)/shard_map/psum | solution.py:67
  109.7 50.5 %copy-start.1 = (bf16[1024,512]{1,0:T(8,128)(2,1)S(1)}, bf16[1024,512]{1,0:T(8,128)(2,1)}, u32[]{:S(2)}) copy-start(bf16[1024,512]{1,0:T(8,128)(2,1)} %param.12) | copy-start | bytes 3145732
  124.5 35.8 %copy-start.2 = (bf16[1024,512]{1,0:T(8,128)(2,1)S(1)}, bf16[1024,512]{1,0:T(8,128)(2,1)}, u32[]{:S(2)}) copy-start(bf16[1024,512]{1,0:T(8,128)(2,1)} %reduce-scatter.2.cloned.1.call-done) | copy-start | bytes 3145732
Sparse Core Ops, SparseCore 0:
  8.9 37.2 all-gather.1
  80.0 44.3 reduce-scatter.1
  127.1 31.7 all-reduce.2
